TPU v7x, 32 devices: a whole 2x2x4 slice. The times are simulated.
32 devices in a mesh: row: 4 (over x, core), col: 8 (over z, y).
Axes of the slice: x: 2, y: 2, z: 4, core: 2. Of those that a mesh axis runs over, the one named last changes fastest.
Arguments:
- momentum: float32 [5120, 27648], P('row', 'col'), may hold values from -130 to 130, as said below
- activations: bfloat16 [2048, 5120], P(None, 'row'), may hold values from -6 to 6
- out_grads: bfloat16 [2048, 27648], P(None, 'col'), may hold values from -0.125 to 0.125
- basis: float32 [27648, 256], P('col'), may hold values from -6 to 6
Outputs:
- new_momentum: float32 [5120, 27648], P('row', 'col')
- left_basis: float32 [5120, 256], P('row')
- new_basis: float32 [27648, 256], P('col')
Inputs may be any that keep to these rules, and one draw needn't show every extreme that they name: `momentum`: Real-valued entries of order one with varying row and column scales.
All inputs are finite; a program needn't handle non-finite values.
Results may differ from a plain program's by a relative error of at most 0.0003.
Values sent between devices are 32-bit elements; how exact they have to be, the bound alone decides.
No kernel may reach another device: no remote copies, remote signals or barrier semaphores. Data moves between devices by JAX's collectives and lax.ppermute only.
A program may use at most 128 MiB of HBM per device.

v0:
```python
import math
import jax
import jax.numpy as jnp
from jax import lax
from jax.sharding import PartitionSpec as P

D = 5120
F = 27648
EPS = 1e-06
HIGH = lax.Precision.HIGHEST


def left_product(block, factor_rows):
    return lax.dot_general(
        block,
        factor_rows,
        (((0,), (0,)), ((), ())),
        precision=HIGH,
        preferred_element_type=jnp.float32,
    )


def invert_gram(gram_total):
    factor = jnp.linalg.cholesky(gram_total)
    identity = jnp.eye(factor.shape[0], dtype=jnp.float32)
    return jax.scipy.linalg.solve_triangular(factor, identity, lower=True).T


def shards(momentum, activations, out_grads, basis):
    gradient = lax.dot_general(
        activations, out_grads, (((0,), (0,)), ((), ())), preferred_element_type=jnp.float32
    )
    merged = momentum + gradient
    block_rows = lax.psum(jnp.dot(merged, basis, precision=HIGH), "col")
    gram_part = jnp.dot(block_rows.T, block_rows, precision=HIGH)
    gram_total = lax.psum(gram_part, "row")
    inverse_t = invert_gram(gram_total)
    ortho = jnp.dot(block_rows, inverse_t, precision=HIGH)
    coeff_part = left_product(merged, ortho)
    coeffs = lax.psum(coeff_part, "row")
    squares = jnp.sum(coeffs * coeffs, axis=0)
    sq_total = lax.psum(squares, "col")
    new_momentum = merged - 0.5 * jnp.dot(ortho, coeffs.T, precision=HIGH)
    inv_norm = lax.rsqrt(sq_total / F + EPS)
    new_basis = coeffs * inv_norm[None, :]
    left_basis = ortho * jnp.float32(math.sqrt(D))
    return (new_momentum, left_basis, new_basis)


def solution(mesh):
    return jax.shard_map(
        shards,
        mesh=mesh,
        in_specs=(P("row", "col"), P(None, "row"), P(None, "col"), P("col", None)),
        out_specs=(P("row", "col"), P("row", None), P("col", None)),
        check_vma=False,
    )
```

profile of v0, /device:TPU:0, one launch (start us, length us, event | category | flops | bytes accessed | tf_op | source)
XLA Modules:
  0.0 406.0 jit_solution(12141631374180239289)
XLA Ops:
  7.2 0.0 copy-start
  7.2 0.0 all-reduce.5.cloned.1.call-start
  7.2 29.5 %convolution_add_fusion = f32[1280,3456]{1,0:T(8,128)} fusion(f32[1280,3456]{1,0:T(8,128)} %param.4, bf16[2048,1280]{1,0:T(8,128)(2,1)} %param.5, bf16[2048,3456]{1,0:T(8,128)(2,1)} %param.6), kind=kOutput, calls=%fused_computation.2 | convolution fusion | flops 18123816960 | bytes 54788096 | tf_op jit(solution)/shard_map/dot_general | solution.py:30
  36.7 0.0 copy-done
  36.7 18.5 %fusion.15 = f32[1280,256]{1,0:T(8,128)} fusion(f32[1280,3456]{1,0:T(8,128)} %convolution_add_fusion, f32[3456,256]{1,0:T(8,128)S(1)} %copy-done), kind=kOutput, calls=%fused_computation.41 | convolution fusion | flops 13589544960 | bytes 22544384 | tf_op jit(solution)/shard_map/dot_general | solution.py:34
  55.2 0.0 all-reduce.5.cloned.1.call-update
  55.2 0.2 all-reduce.7.cloned.1.call-start
  55.4 86.3 %all-reduce.5.cloned.1.call-done = f32[1280,256]{1,0:T(8,128)} async-done(((f32[1280,256]{1,0:T(8,128)}), f32[1280,256]{1,0:T(8,128)}) %all-reduce.5.cloned.1.call-update) | async-done | bytes 1310736 | tf_op jit(solution)/shard_map/psum | solution.py:34
  141.7 0.0 copy-start.4
  141.7 4.7 %fusion.16 = f32[256,256]{0,1:T(8,128)} fusion(f32[1280,256]{1,0:T(8,128)} %all-reduce.5.cloned.1.call-done), kind=kOutput, calls=%fused_computation.42 | convolution fusion | flops 1006632960 | bytes 1572864 | tf_op jit(solution)/shard_map/dot_general | solution.py:35
  146.4 0.0 all-reduce.7.cloned.1.call-update
  146.5 0.0 all-reduce.9.cloned.1.call-start
  146.6 31.4 %all-reduce.7.cloned.1.call-done = f32[256,256]{0,1:T(8,128)} async-done(((f32[256,256]{0,1:T(8,128)}), f32[256,256]{0,1:T(8,128)}) %all-reduce.7.cloned.1.call-update) | async-done | bytes 262160 | tf_op jit(solution)/shard_map/psum | solution.py:36
  178.0 1.1 copy.8
  179.0 1.0 fusion.5
  180.0 11.7 %cholesky.50 = f32[128,128]{1,0:T(8,128)S(1)} custom-call(f32[128,128]{1,0:T(8,128)S(1)} %cholesky.118), custom_call_target="Cholesky" | custom-call | tf_op jit(solution)/shard_map/jit(cholesky)/cholesky | solution.py:24
  191.8 9.8 %custom-call.15 = f32[1,128,128]{1,2,0:T(8,128)S(1)} custom-call(f32[1,128,128]{2,1,0:T(8,128)S(1)} %get-tuple-element.24), custom_call_target="InvertDiagBlocksLowerTriangular" | custom-call | tf_op jit(solution)/shard_map/jit(cholesky)/cholesky | solution.py:24
  201.6 0.2 constant_dynamic-update-slice_fusion.1
  201.9 0.3 convolution_subtract_fusion.1
  202.1 11.7 %cholesky.105 = f32[128,128]{1,0:T(8,128)S(1)} custom-call(f32[128,128]{1,0:T(8,128)S(1)} %convolution_subtract_fusion.1), custom_call_target="Cholesky" | custom-call | tf_op jit(solution)/shard_map/jit(cholesky)/cholesky | solution.py:24
  213.9 0.7 compare_reduce_fusion
  215.9 0.1 triangular_solve.63
  215.9 4.2 %while.1 = (s32[]{:T(128)}, f32[256,256]{1,0:T(8,128)S(1)}, s32[2,2]{1,0:T(2,128)S(1)}, f32[2,128,128]{2,1,0:T(8,128)S(1)}, s32[]{:T(128)}) while((s32[]{:T(128)}, f32[256,256]{1,0:T(8,128)S(1)}, s32[2,2]{1,0:T(2,128)S(1)}, f32[2,128,128]{2,1,0:T(8,128)S(1)}, s32[]{:T(128)}) %tuple.28), condition=%wide.while_cond, body=%wide.while_body.sunk | while | flops 2 | bytes 131189 | solution.py:26
  216.2 0.6 fusion.34
  216.7 1.4 bitcast_dynamic-update-slice_fusion.2
  218.1 0.6 fusion.34
  218.7 1.4 bitcast_dynamic-update-slice_fusion.2
  220.1 19.7 %custom-call.16 = f32[2,128,128]{1,2,0:T(8,128)S(1)} custom-call(f32[2,128,128]{2,1,0:T(8,128)S(1)} %get-tuple-element.10), custom_call_target="InvertDiagBlocksLowerTriangular" | custom-call | tf_op jit(solution)/shard_map/jit(_solve_triangular)/triangular_solve | solution.py:26
  239.8 0.3 fusion.6
  240.1 0.3 convolution_subtract_fusion
  240.3 0.3 fusion.9
  240.7 0.0 copy-done.4
  240.7 2.3 broadcast_multiply_fusion.1
  242.9 0.0 copy-start.3
  242.9 32.2 %fusion.17 = f32[3456,256]{1,0:T(8,128)} fusion(f32[1280,3456]{1,0:T(8,128)} %convolution_add_fusion, f32[1280,256]{1,0:T(8,128)S(1)} %get-tuple-element.28), kind=kOutput, calls=%fused_computation.43 | convolution fusion | flops 13589544960 | bytes 22544384 | tf_op jit(solution)/shard_map/dot_general | solution.py:14
  275.1 0.0 copy-done.3
  275.1 0.0 all-reduce.9.cloned.1.call-update
  275.2 75.0 %all-reduce.9.cloned.1.call-done = f32[3456,256]{1,0:T(8,128)} async-done(((f32[3456,256]{1,0:T(8,128)}), f32[3456,256]{1,0:T(8,128)}) %all-reduce.9.cloned.1.call-update) | async-done | bytes 3538960 | tf_op jit(solution)/shard_map/psum | solution.py:40
  350.1 2.5 multiply_reduce_fusion
  352.6 21.6 %psum.31 = f32[256]{0:T(256)S(1)} all-reduce(f32[256]{0:T(256)S(1)} %multiply_reduce_fusion), channel_id=1, replica_groups=mesh['row'=4,'col'=8] {'col'}, use_global_device_ids=true, to_apply=%region_8.9 | all-reduce | flops 256 | bytes 2048 | tf_op jit(solution)/shard_map/psum | solution.py:42
  374.2 0.0 copy-start.2
  374.2 0.0 copy-start.1
  374.2 22.7 %fusion = f32[1280,3456]{1,0:T(8,128)} fusion(f32[1280,3456]{1,0:T(8,128)} %convolution_add_fusion, f32[1280,256]{1,0:T(8,128)} %copy-done.3, f32[3456,256]{1,0:T(8,128)} %all-reduce.9.cloned.1.call-done), kind=kOutput, calls=%fused_computation.4 | convolution fusion | flops 13598392320 | bytes 40239104 | tf_op jit(solution)/shard_map/dot_general | solution.py:43
  397.0 0.0 copy-done.2
  397.0 2.0 broadcast_multiply_fusion
  399.0 0.0 copy-done.1
  (11 shorter events, 0.2 us)
Async XLA Ops:
  7.2 29.5 %copy-start = (f32[3456,256]{1,0:T(8,128)S(1)}, f32[3456,256]{1,0:T(8,128)}, u32[]{:S(2)}) copy-start(f32[3456,256]{1,0:T(8,128)} %param.7) | copy-start | bytes 10616836
  7.2 134.5 %all-reduce.5.cloned.1.call-start = ((), (), s32[]{:S(2)}) async-start(), calls=%async_computation | async-start | bytes 2621440 | tf_op jit(solution)/shard_map/psum | solution.py:34
  55.2 122.8 %all-reduce.7.cloned.1.call-start = ((), (), s32[]{:S(2)}) async-start(), calls=%async_computation.1 | async-start | bytes 524288 | tf_op jit(solution)/shard_map/psum | solution.py:36
  141.7 99.0 %copy-start.4 = (f32[1280,256]{1,0:T(8,128)S(1)}, f32[1280,256]{1,0:T(8,128)}, u32[]{:S(2)}) copy-start(f32[1280,256]{1,0:T(8,128)} %all-reduce.5.cloned.1.call-done) | copy-start | bytes 3932164
  146.5 203.7 %all-reduce.9.cloned.1.call-start = ((), (), s32[]{:S(2)}) async-start(), calls=%async_computation.2 | async-start | bytes 7077888 | tf_op jit(solution)/shard_map/psum | solution.py:40
  242.9 32.2 %copy-start.3 = (f32[1280,256]{1,0:T(8,128)}, f32[1280,256]{1,0:T(8,128)S(1)}, u32[]{:S(2)}) copy-start(f32[1280,256]{1,0:T(8,128)S(1)} %get-tuple-element.28) | copy-start | bytes 3932164
  374.2 22.7 %copy-start.2 = (f32[3456,256]{1,0:T(8,128)S(1)}, f32[3456,256]{1,0:T(8,128)}, u32[]{:S(2)}) copy-start(f32[3456,256]{1,0:T(8,128)} %all-reduce.9.cloned.1.call-done) | copy-start | bytes 10616836
  374.2 24.8 %copy-start.1 = (f32[3456,256]{1,0:T(8,128)S(1)}, f32[3456,256]{1,0:T(8,128)}, u32[]{:S(2)}) copy-start(f32[3456,256]{1,0:T(8,128)} %param.7) | copy-start | bytes 10616836
Sparse Core Ops, SparseCore 0:
  55.3 86.3 all-reduce.4
  146.6 31.3 all-reduce.6
  275.3 74.8 all-reduce.8
where the time goes:
time: 414 us; the launch traced here: 406 us
  waiting for transfers between devices  193 us (47%)
  matrix products  111 us (27%)
  other arithmetic  59.2 us (14%)
  blocking collectives  21.6 us (5%)
  between operations  15.6 us (4%)
  local copies, waits for them, and re-layouts  5.12 us (1%)
    psum x1, waiting for transfers between devices, shards(): block_rows = lax.psum(jnp.dot(merged, basis, precision=HIGH), 'col')  86.3 us
    psum x1, waiting for transfers between devices, shards(): coeffs = lax.psum(coeff_part, 'row')  75 us
    another operation x6, other arithmetic, invert_gram(): factor = jnp.linalg.cholesky(gram_total)  34 us
    dot_general x1, matrix products, left_product(): lax.dot_general(block, factor_rows, (((0,), (0,)), ((), ())), precision=H...  32.2 us
    psum x1, waiting for transfers between devices, shards(): gram_total = lax.psum(gram_part, 'row')  31.4 us
    dot_general x1, matrix products, shards(): lax.dot_general(activations, out_grads, (((0,), (0,)), ((), ())), preferr...  29.5 us
    dot_general x1, matrix products, shards(): new_momentum = merged - 0.5 * jnp.dot(ortho, coeffs.T, precision=HIGH)  22.7 us
    psum x1, blocking collectives, shards(): sq_total = lax.psum(squares, 'col')  21.6 us
  transfers between devices with their start and end apart: 3, of which 3 were waited for; matrix products, arithmetic and copies ran while one was open for 0% of the time, Pallas kernels for 0%

commit v1 on v0

--- a/solution.py
+++ b/solution.py
@@ -37,7 +37,9 @@
     inverse_t = invert_gram(gram_total)
     ortho = jnp.dot(block_rows, inverse_t, precision=HIGH)
     coeff_part = left_product(merged, ortho)
-    coeffs = lax.psum(coeff_part, "row")
+    coeffs = coeff_part
+    for hop in (1, 2):
+        coeffs = coeffs + lax.ppermute(coeffs, "row", [(dev, dev ^ hop) for dev in range(4)])
     squares = jnp.sum(coeffs * coeffs, axis=0)
     sq_total = lax.psum(squares, "col")
     new_momentum = merged - 0.5 * jnp.dot(ortho, coeffs.T, precision=HIGH)

time: 414 us -> 421 us (1.017)
  waiting for transfers between devices: 193 us -> 202 us
    ppermute x0 -> x2, waiting for transfers between devices: none -> 84.7 us  [shards(): lax.ppermute(coeffs, 'row', [(dev, dev ^ hop) for dev in range(4)])]
    psum x1 -> x0, waiting for transfers between devices: 75 us -> none  [shards(): coeffs = lax.psum(coeff_part, 'row')]
  transfers between devices with their start and end apart: 3 -> 4, of which waited for: 3 -> 4; matrix products, arithmetic and copies ran while one was open for 0% -> 0% of each run, Pallas kernels for 0% -> 0%
where the time goes in v1:
time: 421 us; the launch traced here: 413 us
  waiting for transfers between devices  202 us (48%)
  matrix products  107 us (25%)
  other arithmetic  60.4 us (14%)
  blocking collectives  21.3 us (5%)
  between operations  16 us (4%)
  local copies, waits for them, and re-layouts  5.23 us (1%)
    psum x1, waiting for transfers between devices, shards(): block_rows = lax.psum(jnp.dot(merged, basis, precision=HIGH), 'col')  86.3 us
    ppermute x2, waiting for transfers between devices, shards(): lax.ppermute(coeffs, 'row', [(dev, dev ^ hop) for dev in range(4)])  84.7 us
    another operation x6, other arithmetic, invert_gram(): factor = jnp.linalg.cholesky(gram_total)  34.2 us
    psum x1, waiting for transfers between devices, shards(): gram_total = lax.psum(gram_part, 'row')  31.4 us
    dot_general x1, matrix products, left_product(): lax.dot_general(block, factor_rows, (((0,), (0,)), ((), ())), precision=H...  30.9 us
    dot_general x1, matrix products, shards(): lax.dot_general(activations, out_grads, (((0,), (0,)), ((), ())), preferr...  29.5 us
    psum x1, blocking collectives, shards(): sq_total = lax.psum(squares, 'col')  21.3 us
    another operation x3, other arithmetic, invert_gram(): return jax.scipy.linalg.solve_triangular(factor, identity, lower=True).T  19.7 us
  transfers between devices with their start and end apart: 4, of which 4 were waited for; matrix products, arithmetic and copies ran while one was open for 0% of the time, Pallas kernels for 0%

profile of v1, /device:TPU:0, one launch (start us, length us, event | category | flops | bytes accessed | tf_op | source)
XLA Modules:
  0.0 412.8 jit_solution(16189179372167860639)
XLA Ops:
  7.2 0.0 copy-start
  7.2 0.0 all-reduce.4.cloned.1.call-start
  7.2 29.5 %convolution_add_fusion = f32[1280,3456]{1,0:T(8,128)} fusion(f32[1280,3456]{1,0:T(8,128)} %param.4, bf16[2048,1280]{1,0:T(8,128)(2,1)} %param.5, bf16[2048,3456]{1,0:T(8,128)(2,1)} %param.6), kind=kOutput, calls=%fused_computation.2 | convolution fusion | flops 18123816960 | bytes 54788096 | tf_op jit(solution)/shard_map/dot_general | solution.py:30
  36.7 0.0 copy-done
  36.7 18.5 %fusion.15 = f32[1280,256]{1,0:T(8,128)} fusion(f32[1280,3456]{1,0:T(8,128)} %convolution_add_fusion, f32[3456,256]{1,0:T(8,128)S(1)} %copy-done), kind=kOutput, calls=%fused_computation.41 | convolution fusion | flops 13589544960 | bytes 22544384 | tf_op jit(solution)/shard_map/dot_general | solution.py:34
  55.2 0.0 all-reduce.4.cloned.1.call-update
  55.2 0.2 all-reduce.6.cloned.1.call-start
  55.4 86.3 %all-reduce.4.cloned.1.call-done = f32[1280,256]{1,0:T(8,128)} async-done(((f32[1280,256]{1,0:T(8,128)}), f32[1280,256]{1,0:T(8,128)}) %all-reduce.4.cloned.1.call-update) | async-done | bytes 1310736 | tf_op jit(solution)/shard_map/psum | solution.py:34
  141.7 4.8 %fusion.16 = f32[256,256]{0,1:T(8,128)} fusion(f32[1280,256]{1,0:T(8,128)} %all-reduce.4.cloned.1.call-done), kind=kOutput, calls=%fused_computation.42 | convolution fusion | flops 1006632960 | bytes 1572864 | tf_op jit(solution)/shard_map/dot_general | solution.py:35
  146.5 0.0 all-reduce.6.cloned.1.call-update
  146.6 31.4 %all-reduce.6.cloned.1.call-done = f32[256,256]{0,1:T(8,128)} async-done(((f32[256,256]{0,1:T(8,128)}), f32[256,256]{0,1:T(8,128)}) %all-reduce.6.cloned.1.call-update) | async-done | bytes 262160 | tf_op jit(solution)/shard_map/psum | solution.py:36
  178.0 1.1 copy.8
  179.1 1.0 fusion.5
  180.1 11.7 %cholesky.50 = f32[128,128]{1,0:T(8,128)S(1)} custom-call(f32[128,128]{1,0:T(8,128)S(1)} %cholesky.118), custom_call_target="Cholesky" | custom-call | tf_op jit(solution)/shard_map/jit(cholesky)/cholesky | solution.py:24
  191.8 9.8 %custom-call.15 = f32[1,128,128]{1,2,0:T(8,128)S(1)} custom-call(f32[1,128,128]{2,1,0:T(8,128)S(1)} %get-tuple-element.26), custom_call_target="InvertDiagBlocksLowerTriangular" | custom-call | tf_op jit(solution)/shard_map/jit(cholesky)/cholesky | solution.py:24
  201.7 0.2 constant_dynamic-update-slice_fusion.1
  201.9 0.3 convolution_subtract_fusion.1
  202.2 11.9 %cholesky.105 = f32[128,128]{1,0:T(8,128)S(1)} custom-call(f32[128,128]{1,0:T(8,128)S(1)} %convolution_subtract_fusion.1), custom_call_target="Cholesky" | custom-call | tf_op jit(solution)/shard_map/jit(cholesky)/cholesky | solution.py:24
  214.1 0.7 compare_reduce_fusion
  216.2 0.1 triangular_solve.63
  216.2 4.0 while.1
  216.2 0.6 fusion.34
  216.8 1.4 bitcast_dynamic-update-slice_fusion.2
  218.3 0.6 fusion.34
  218.9 1.4 bitcast_dynamic-update-slice_fusion.2
  220.3 19.7 %custom-call.16 = f32[2,128,128]{1,2,0:T(8,128)S(1)} custom-call(f32[2,128,128]{2,1,0:T(8,128)S(1)} %get-tuple-element.10), custom_call_target="InvertDiagBlocksLowerTriangular" | custom-call | tf_op jit(solution)/shard_map/jit(_solve_triangular)/triangular_solve | solution.py:26
  240.0 0.3 fusion.6
  240.2 0.3 convolution_subtract_fusion
  240.5 0.3 fusion.9
  240.8 0.0 copy-done.3
  240.8 2.3 broadcast_multiply_fusion.1
  243.1 30.9 %fusion.17 = f32[3456,256]{1,0:T(8,128)S(1)} fusion(f32[1280,3456]{1,0:T(8,128)} %convolution_add_fusion, f32[1280,256]{1,0:T(8,128)S(1)} %get-tuple-element.30), kind=kOutput, calls=%fused_computation.43 | convolution fusion | flops 13589544960 | bytes 22544384 | tf_op jit(solution)/shard_map/dot_general | solution.py:14
  274.1 0.0 slice-start.3
  274.1 0.1 collective-permute-start
  274.2 6.2 %collective-permute-done = f32[3456,256]{1,0:T(8,128)S(1)} collective-permute-done((f32[3456,256]{1,0:T(8,128)S(1)}, f32[3456,256]{1,0:T(8,128)S(1)}, u32[]{:S(2)}, u32[]{:S(2)}) %collective-permute-start) | collective-permute-done | bytes 3538976 | tf_op jit(solution)/shard_map/ppermute | solution.py:42
  280.4 0.5 add.46
  280.8 0.0 slice-start.4
  280.8 0.1 collective-permute-start.1
  280.9 78.5 %collective-permute-done.1 = f32[3456,256]{1,0:T(8,128)S(1)} collective-permute-done((f32[3456,256]{1,0:T(8,128)S(1)}, f32[3456,256]{1,0:T(8,128)S(1)}, u32[]{:S(2)}, u32[]{:S(2)}) %collective-permute-start.1) | collective-permute-done | bytes 3538976 | tf_op jit(solution)/shard_map/ppermute | solution.py:42
  359.5 0.8 multiply_reduce_fusion
  360.3 0.0 slice-done
  360.3 0.0 slice-done.1
  360.3 0.0 slice-done.2
  360.4 0.0 slice-done.3
  360.4 0.0 slice-done.4
  360.4 19.6 %fusion = f32[1280,3456]{1,0:T(8,128)} fusion(f32[1280,3456]{1,0:T(8,128)S(1)} %bitcast.43, f32[1280,256]{1,0:T(8,128)S(1)} %get-tuple-element.30, f32[3456,256]{1,0:T(8,128)S(1)} %get-tuple-element.20), kind=kOutput, calls=%fused_computation.4 | convolution fusion | flops 13598392320 | bytes 40239104 | tf_op jit(solution)/shard_map/dot_general | solution.py:45
  380.0 21.3 %psum.23 = f32[256]{0:T(256)S(1)} all-reduce(f32[256]{0:T(256)S(1)} %get-tuple-element.19), channel_id=1, replica_groups=mesh['row'=4,'col'=8] {'col'}, use_global_device_ids=true, to_apply=%region_7.8 | all-reduce | flops 256 | bytes 2048 | tf_op jit(solution)/shard_map/psum | solution.py:44
  401.3 4.2 %broadcast_multiply_fusion = f32[3456,256]{1,0:T(8,128)} fusion(f32[3456,256]{1,0:T(8,128)} %copy-done.2, f32[256]{0:T(256)S(1)} %add_rsqrt_fusion), kind=kLoop, calls=%fused_computation.6 | loop fusion | flops 884736 | bytes 7078912 | tf_op jit(solution)/shard_map/mul | solution.py:47
  (20 shorter events, 0.2 us)
Async XLA Ops:
  7.2 29.5 %copy-start = (f32[3456,256]{1,0:T(8,128)S(1)}, f32[3456,256]{1,0:T(8,128)}, u32[]{:S(2)}) copy-start(f32[3456,256]{1,0:T(8,128)} %param.7) | copy-start | bytes 10616836
  7.2 134.5 %all-reduce.4.cloned.1.call-start = ((), (), s32[]{:S(2)}) async-start(), calls=%async_computation | async-start | bytes 2621440 | tf_op jit(solution)/shard_map/psum | solution.py:34
  55.2 122.8 %all-reduce.6.cloned.1.call-start = ((), (), s32[]{:S(2)}) async-start(), calls=%async_computation.1 | async-start | bytes 524288 | tf_op jit(solution)/shard_map/psum | solution.py:36
  141.7 99.1 %copy-start.3 = (f32[1280,256]{1,0:T(8,128)S(1)}, f32[1280,256]{1,0:T(8,128)}, u32[]{:S(2)}) copy-start(f32[1280,256]{1,0:T(8,128)} %all-reduce.4.cloned.1.call-done) | copy-start | bytes 3932164
  243.1 117.2 %slice-start = ((s8[17694720]{0:T(1024)(128)(4,1)}), s8[4194304]{0:T(1024)(128)(4,1)S(1)}, s32[]{:S(2)}) async-start(s8[17694720]{0:T(1024)(128)(4,1)} %bitcast.42), calls=%async_computation.2 | async-start | bytes 8388608
  243.1 117.2 %slice-start.1 = ((s8[17694720]{0:T(1024)(128)(4,1)}), s8[4194304]{0:T(1024)(128)(4,1)S(1)}, s32[]{:S(2)}) async-start(s8[17694720]{0:T(1024)(128)(4,1)} %bitcast.42), calls=%async_computation.3 | async-start | bytes 8388608
  243.1 117.2 %slice-start.2 = ((s8[17694720]{0:T(1024)(128)(4,1)}), s8[4194304]{0:T(1024)(128)(4,1)S(1)}, s32[]{:S(2)}) async-start(s8[17694720]{0:T(1024)(128)(4,1)} %bitcast.42), calls=%async_computation.4 | async-start | bytes 8388608
  274.1 86.3 %slice-start.3 = ((s8[17694720]{0:T(1024)(128)(4,1)}), s8[4194304]{0:T(1024)(128)(4,1)S(1)}, s32[]{:S(2)}) async-start(s8[17694720]{0:T(1024)(128)(4,1)} %bitcast.42), calls=%async_computation.5 | async-start | bytes 8388608
  274.1 6.3 %collective-permute-start = (f32[3456,256]{1,0:T(8,128)S(1)}, f32[3456,256]{1,0:T(8,128)S(1)}, u32[]{:S(2)}, u32[]{:S(2)}) collective-permute-start(f32[3456,256]{1,0:T(8,128)S(1)} %fusion.17), channel_id=1, source_target_pairs={{0,8},{8,0},{16,24},{24,16},{1,9},{9,1},{17,25},{25,17},{2,10},{10... | collective-permute-start | bytes 10616840 | tf_op jit(solution)/shard_map/ppermute | solution.py:42
  280.8 79.5 %slice-start.4 = ((s8[17694720]{0:T(1024)(128)(4,1)}), s8[917504]{0:T(1024)(128)(4,1)S(1)}, s32[]{:S(2)}) async-start(s8[17694720]{0:T(1024)(128)(4,1)} %bitcast.42), calls=%async_computation.6 | async-start | bytes 1835008
  280.8 78.6 %collective-permute-start.1 = (f32[3456,256]{1,0:T(8,128)S(1)}, f32[3456,256]{1,0:T(8,128)S(1)}, u32[]{:S(2)}, u32[]{:S(2)}) collective-permute-start(f32[3456,256]{1,0:T(8,128)S(1)} %add.46), channel_id=1, source_target_pairs={{0,16},{8,24},{16,0},{24,8},{1,17},{9,25},{17,1},{25,9},{2,18},{10... | collective-permute-start | bytes 10616840 | tf_op jit(solution)/shard_map/ppermute | solution.py:42
  360.3 19.7 %copy-start.2 = (f32[3456,256]{1,0:T(8,128)}, f32[3456,256]{1,0:T(8,128)S(1)}, u32[]{:S(2)}) copy-start(f32[3456,256]{1,0:T(8,128)S(1)} %get-tuple-element.20) | copy-start | bytes 10616836
  401.3 4.2 %copy-start.1 = (f32[3456,256]{1,0:T(8,128)S(1)}, f32[3456,256]{1,0:T(8,128)}, u32[]{:S(2)}) copy-start(f32[3456,256]{1,0:T(8,128)} %param.7) | copy-start | bytes 10616836
Sparse Core Ops, SparseCore 0:
  55.3 86.3 all-reduce.3
  146.6 31.3 all-reduce.5
